TPU v7x, 32 devices: a whole 2x2x4 slice. The times are simulated.
32 devices in a mesh: dp: 8 (over y, x, core), tm: 4 (over z).
Axes of the slice: x: 2, y: 2, z: 4, core: 2. Of those that a mesh axis runs over, the one named last changes fastest.
Arguments:
- tokens: bfloat16 [8, 4, 256, 1024], P('dp', 'tm'), may hold values from -6 to 6
- gain: bfloat16 [1024], replicated, may hold values from 0.25 to 1.75
- w_qkv: bfloat16 [1024, 3072], P('dp'), may hold values from -0.1875 to 0.1875
- w_out: bfloat16 [1024, 1024], P('dp'), may hold values from -0.1875 to 0.1875
- w_pair: float32 [2, 1024, 32], replicated, may hold values from -3 to 3
- codebook: float32 [8, 32], replicated, may hold values from -5 to 5
- codes: int32 [8, 4, 1], P('dp', 'tm'), may hold values from 0 to 7
Outputs:
- grad_tokens: bfloat16 [8, 4, 256, 1024], P('dp', 'tm')
- grad_pair: float32 [2, 1024, 32], replicated
- codebook_step: float32 [8, 32], replicated
Inputs may be any that keep to these rules, and one draw needn't show every extreme that they name: Every one of the 8 codes is assigned to some clip frame.
All inputs are finite; a program needn't handle non-finite values.
Results may differ from a plain program's by a relative error of at most 0.014.
Values may be sent and summed in bfloat16 or wider, within the bound.
A program may use at most 64 MiB of HBM per device.

v0:
```python
import jax
import jax.numpy as jnp
from jax import lax
from jax.sharding import PartitionSpec as P

D = 1024
HEAD_DIM = 64
CODES = 8
PATCHES = 256
EPS = 1e-06
BETA = 0.25


def passed_along(value, axis, by):
    count = lax.axis_size(axis)
    pairs = [(i, i + by) for i in range(count) if 0 <= i + by < count]
    return lax.ppermute(value, axis, pairs)


def normalize(xf, gain):
    scale = lax.rsqrt(jnp.mean(xf * xf, axis=-1, keepdims=True) + EPS)
    return (xf * scale * gain.astype(jnp.float32)).astype(jnp.bfloat16)


def project(normed, weight):
    shape = normed.shape
    flat = jnp.dot(normed.reshape(-1, shape[-1]), weight, preferred_element_type=jnp.float32)
    return flat.astype(jnp.bfloat16).reshape(shape[:-1] + (3, shape[-1]))


def attend(qkv):
    clips, frames, patches, _, width = qkv.shape
    local_heads = width // HEAD_DIM
    parts = qkv.reshape(clips, frames, patches, 3, local_heads, HEAD_DIM)
    query = parts[:, :, :, 0].astype(jnp.float32)
    keys = parts[:, :, :, 1].astype(jnp.float32)
    values = parts[:, :, :, 2].astype(jnp.float32)
    scores = jnp.einsum("cfphd,cgphd->cphfg", query, keys) * HEAD_DIM ** (-0.5)
    causal = jnp.arange(frames)[:, None] >= jnp.arange(frames)[None, :]
    scores = jnp.where(causal, scores, -1e30)
    weights = jax.nn.softmax(scores, axis=-1).astype(jnp.bfloat16)
    mixed = jnp.einsum("cphfg,cgphd->cfphd", weights.astype(jnp.float32), values)
    return mixed.reshape(clips, frames, patches, width).astype(jnp.bfloat16)


def output(xf, attended, weight):
    shape = xf.shape
    moved = jnp.dot(attended.reshape(-1, shape[-1]), weight, preferred_element_type=jnp.float32)
    return jnp.mean(xf + moved.reshape(shape), axis=2)


def local(tokens, gain, w_qkv, w_out, w_pair, codebook, codes):
    xf = tokens.astype(jnp.float32)
    groups = lax.axis_size("tm")
    full_out = w_out
    full_qkv, full_out = (
        lax.all_gather(w_qkv, "dp", axis=0, tiled=True),
        lax.all_gather(w_out, "dp", axis=0, tiled=True),
    )
    normed, norm_back = jax.vjp(lambda value: normalize(value, gain), xf)
    regrouped = lax.all_to_all(normed, "tm", split_axis=2, concat_axis=1, tiled=True)
    qkv, qkv_back = jax.vjp(lambda value: project(value, full_qkv), regrouped)
    attended, attend_back = jax.vjp(attend, qkv)
    lifted = attended[:, :, None]
    returned = lax.all_to_all(lifted, "tm", split_axis=1, concat_axis=2, tiled=True)
    clips_here, frames_here = (returned.shape[0], returned.shape[1])
    local_out = returned.reshape(clips_here, frames_here, -1, D)
    pooled, out_back = jax.vjp(lambda first, second: output(first, second, full_out), xf, local_out)
    following = passed_along(pooled, "tm", -1)
    flat_now = pooled.reshape(-1, D)
    flat_next = following.reshape(-1, D)
    highest = lax.Precision.HIGHEST
    action = jnp.dot(flat_now, w_pair[0], precision=highest) + jnp.dot(
        flat_next, w_pair[1], precision=highest
    )
    onehot = (codes.reshape(-1)[:, None] == jnp.arange(CODES)[None, :]).astype(jnp.float32)
    quantized = jnp.dot(onehot, codebook, precision=highest)
    diff = action - quantized
    d_action = 2.0 * BETA * diff
    d_quant = -2.0 * diff
    pair_part = jnp.stack(
        [
            jnp.dot(flat_now.T, d_action, precision=highest),
            jnp.dot(flat_next.T, d_action, precision=highest),
        ]
    )
    code_part = jnp.dot(onehot.T, d_quant, precision=highest)
    count_part = jnp.sum(onehot, axis=0)
    grad_pair, code_total, count = lax.psum((pair_part, code_part, count_part), ("dp", "tm"))
    codebook_step = code_total / count[:, None]
    d_own = jnp.dot(d_action, w_pair[0].T, precision=highest).reshape(pooled.shape)
    d_next = jnp.dot(d_action, w_pair[1].T, precision=highest).reshape(pooled.shape)
    carried = passed_along(d_next, "tm", 1)
    d_pooled = (d_own + carried) * PATCHES
    d_resid, d_local = out_back(d_pooled)
    clips_here, frames_here, rows_here = (d_local.shape[0], d_local.shape[1], d_local.shape[2])
    spread = d_local.reshape(clips_here, frames_here, groups, rows_here // groups, D)
    gathered_back = lax.all_to_all(spread, "tm", split_axis=2, concat_axis=1, tiled=True)
    d_attended = gathered_back.reshape(attended.shape)
    (d_qkv,) = attend_back(d_attended)
    (d_regrouped,) = qkv_back(d_qkv)
    d_normed = lax.all_to_all(d_regrouped, "tm", split_axis=1, concat_axis=2, tiled=True)
    (d_through,) = norm_back(d_normed)
    grad_tokens = (d_resid + d_through).astype(jnp.bfloat16)
    return (grad_tokens, grad_pair, codebook_step)


def solution(mesh):
    placed = (
        P("dp", "tm", None, None),
        P(),
        P("dp", None),
        P("dp", None),
        P(),
        P(),
        P("dp", "tm", None),
    )
    return jax.shard_map(
        local,
        mesh=mesh,
        in_specs=placed,
        out_specs=(P("dp", "tm", None, None), P(), P()),
        check_vma=False,
    )
```

profile of v0, /device:TPU:0, one launch (start us, length us, event | category | flops | bytes accessed | tf_op | source)
XLA Modules:
  0.0 300.7 jit_solution(16761562726995000602)
XLA Ops:
  7.2 0.0 copy-start
  7.2 0.0 all-gather.3.cloned.1.call-start
  7.2 0.7 all-gather.3.cloned.1.call-update
  7.9 0.7 convert_element_type.110
  8.6 1.2 fusion.15
  9.8 1.2 fusion.17
  11.1 0.8 copy.83
  11.9 0.5 broadcast.182
  12.4 3.9 %reduce.9 = bf16[256,1024]{1,0:T(8,128)(2,1)S(1)} reduce(bf16[256,1,1,1024]{3,2,1,0:T(2,128)(2,1)S(1)} %bitcast.152, bf16[]{:T(256)} %broadcast.182), dimensions={1,2}, to_apply=%bitcast.147.reduce_sub_computation | reduce | bytes 1048578
  16.4 1.2 reshape.366
  17.5 6.3 %all-to-all-start = ((bf16[4,2,32768]{2,1,0:T(2,128)(2,1)}), bf16[4,2,32768]{2,1,0:T(2,128)(2,1)S(1)}, u32[]{:S(2)}, u32[]{:S(2)}) async-start(bf16[4,2,32768]{2,1,0:T(2,128)(2,1)} %reshape.366), calls=%async_computation | async-start | bytes 1048576 | tf_op jit(solution)/shard_map/all_to_all | solution.py:61
  23.9 0.7 all-gather.5.cloned.1.call-update
  24.6 13.7 %all-to-all-done = bf16[4,2,32768]{2,1,0:T(2,128)(2,1)S(1)} async-done(((bf16[4,2,32768]{2,1,0:T(2,128)(2,1)}), bf16[4,2,32768]{2,1,0:T(2,128)(2,1)S(1)}, u32[]{:S(2)}, u32[]{:S(2)}) %all-to-all-start) | async-done | bytes 524320 | tf_op jit(solution)/shard_map/all_to_all | solution.py:61
  38.4 0.5 reshape.367
  38.9 19.1 %all-gather.3.cloned.1.call-done = bf16[1024,3072]{1,0:T(8,128)(2,1)} async-done(((bf16[128,3072]{1,0:T(8,128)(2,1)}), bf16[1024,3072]{1,0:T(8,128)(2,1)}) %all-gather.3.cloned.1.call-update) | async-done | bytes 6291472 | tf_op jit(solution)/shard_map/all_gather | solution.py:57
  58.0 5.8 %convolution_convert_fusion = bf16[256,3072]{1,0:T(8,128)(2,1)} fusion(bf16[1024,3072]{1,0:T(8,128)(2,1)} %all-gather.3.cloned.1.call-done, bf16[1,1,256,1024]{3,1,0,2:T(2,128)(2,1)S(1)} %bitcast.154), kind=kOutput, calls=%fused_computation.1 | convolution fusion | flops 1611399168 | bytes 8388608 | tf_op jit(solution)/shard_map/jvp()/dot_general | solution.py:27
  63.8 3.7 %reshape.339 = bf16[1,4,64,3,16,64]{5,4,3,2,1,0:T(8,128)(2,1)S(1)} reshape(bf16[256,3072]{1,0:T(8,128)(2,1)} %convolution_convert_fusion) | data formatting | bytes 3145728 | tf_op jit(solution)/shard_map/jvp()/reshape;jvp()/reshape | solution.py:34
  67.5 1.9 fusion.43
  69.4 5.3 %fusion.44 = (f32[64,16,4]{2,1,0:T(8,128)S(1)}, f32[64,16,4,4]{2,3,1,0:T(4,128)S(1)}) fusion(pred[4,4]{0,1:T(4,128)(4,1)S(1)} %iota_compare_fusion, bf16[1,4,64,1,16,64]{5,4,3,2,1,0:T(8,128)(2,1)} %get-tuple-element.6, bf16[1,4,64,1,16,64]{5,4,3,2,1,0:T(8,128)(2,1)} %get-tuple-element.7), kind=kOutput, calls=%fused_computation.88 | convolution fusion | flops 2162691 | bytes 1130512 | tf_op jit(solution)/shard_map/jvp()/sub | solution.py:41
  74.7 0.6 divide_convert_fusion
  75.4 1.0 copy-done.3
  76.4 1.6 fusion.5
  78.0 0.0 copy-start.1
  78.0 1.2 copy.40
  79.2 2.6 convert_element_type.117
  81.8 4.6 %all-to-all-start.1 = ((bf16[1,4,1,64,1024]{4,3,2,0,1:T(8,128)(2,1)}), bf16[1,4,1,64,1024]{4,3,2,0,1:T(8,128)(2,1)}, u32[]{:S(2)}, u32[]{:S(2)}) async-start(bf16[1,4,1,64,1024]{4,3,2,0,1:T(8,128)(2,1)} %bitcast.153), calls=%async_computation.1 | async-start | bytes 1048576 | tf_op jit(solution)/shard_map/all_to_all | solution.py:65
  87.1 0.1 convolution_bitcast_fusion.3
  87.2 0.5 all-gather.5.cloned.1.call-done
  87.7 13.7 %all-to-all-done.1 = bf16[1,4,1,64,1024]{4,3,2,0,1:T(8,128)(2,1)} async-done(((bf16[1,4,1,64,1024]{4,3,2,0,1:T(8,128)(2,1)}), bf16[1,4,1,64,1024]{4,3,2,0,1:T(8,128)(2,1)}, u32[]{:S(2)}, u32[]{:S(2)}) %all-to-all-start.1) | async-done | bytes 524320 | tf_op jit(solution)/shard_map/all_to_all | solution.py:65
  101.4 2.6 fusion.9
  104.1 1.3 collective-permute-start
  105.4 0.2 convolution_bitcast_fusion.5
  105.6 4.0 %collective-permute-done = f32[1,1,1024]{2,1,0:T(1,128)S(1)} collective-permute-done((f32[1,1,1024]{2,1,0:T(1,128)S(1)}, f32[1,1,1024]{2,1,0:T(1,128)S(1)}, u32[]{:S(2)}, u32[]{:S(2)}) %collective-permute-start) | collective-permute-done | bytes 4128 | tf_op jit(solution)/shard_map/ppermute | solution.py:17
  109.6 0.2 broadcast_multiply_fusion.2
  109.8 0.2 convolution_bitcast_fusion.1
  110.0 1.7 collective-permute-start.1
  111.6 1.3 collective-permute-done.1
  113.0 0.2 fusion.10
  113.2 1.6 convolution_convert_fusion.7
  114.7 3.7 %all-to-all-start.2 = ((bf16[1,1,4,64,1024]{4,3,1,0,2:T(8,128)(2,1)}), bf16[1,1,4,64,1024]{4,3,1,0,2:T(8,128)(2,1)S(1)}, u32[]{:S(2)}, u32[]{:S(2)}) async-start(bf16[1,1,4,64,1024]{4,3,1,0,2:T(8,128)(2,1)} %bitcast.155), calls=%async_computation.2 | async-start | bytes 1048576 | tf_op jit(solution)/shard_map/all_to_all | solution.py:98
  118.4 0.9 multiply_divide_fusion
  119.3 11.2 %all-to-all-done.2 = bf16[1,1,4,64,1024]{4,3,1,0,2:T(8,128)(2,1)S(1)} async-done(((bf16[1,1,4,64,1024]{4,3,1,0,2:T(8,128)(2,1)}), bf16[1,1,4,64,1024]{4,3,1,0,2:T(8,128)(2,1)S(1)}, u32[]{:S(2)}, u32[]{:S(2)}) %all-to-all-start.2) | async-done | bytes 524320 | tf_op jit(solution)/shard_map/all_to_all | solution.py:98
  130.5 1.7 reshape.349
  132.2 2.9 fusion.6
  135.1 2.7 fusion.4
  137.9 1.4 select_multiply_fusion
  139.3 1.2 fusion.7
  140.6 1.6 fusion.8
  142.2 3.1 %pad_add_fusion = bf16[1,4,64,3,16,64]{5,1,4,2,3,0:T(4,128)(2,1)S(1)} fusion(bf16[1,4,64,1,16,64]{5,1,4,2,3,0:T(4,128)(2,1)S(1)} %fusion.8, bf16[1,4,64,1,16,64]{5,1,4,2,3,0:T(4,128)(2,1)S(1)} %fusion.7, bf16[1,4,64,1,16,64]{5,1,4,2,3,0:T(4,128)(2,1)S(1)} %fusion.6), kind=kLoop, calls=%fused_computation.2 | loop fusion | flops 1572864 | bytes 3145728 | tf_op jit(solution)/shard_map/transpose(jvp())/add_any | solution.py:35
  145.4 0.4 copy.45
  145.8 3.2 %reshape.351 = bf16[256,3072]{1,0:T(8,128)(2,1)} reshape(bf16[1,4,64,3,16,64]{5,4,3,2,1,0:T(8,128)(2,1)S(1)} %copy.45) | data formatting | bytes 3145728 | tf_op jit(solution)/shard_map/transpose(jvp())/reshape;transpose(jvp())/reshape | solution.py:28
  149.0 5.9 %convolution_convert_fusion.6 = bf16[256,1024]{1,0:T(8,128)(2,1)} fusion(bf16[256,3072]{1,0:T(8,128)(2,1)} %reshape.351, bf16[1024,3072]{1,0:T(8,128)(2,1)} %all-gather.3.cloned.1.call-done), kind=kOutput, calls=%fused_computation.29 | convolution fusion | flops 1610874880 | bytes 8388608 | tf_op jit(solution)/shard_map/transpose(jvp())/dot_general | solution.py:27
  154.9 3.6 %all-to-all-start.3 = ((bf16[1,4,64,1024]{3,2,0,1:T(8,128)(2,1)}), bf16[1,4,64,1024]{3,2,0,1:T(8,128)(2,1)S(1)}, u32[]{:S(2)}, u32[]{:S(2)}) async-start(bf16[1,4,64,1024]{3,2,0,1:T(8,128)(2,1)} %bitcast.41), calls=%async_computation.3 | async-start | bytes 1048576 | tf_op jit(solution)/shard_map/all_to_all | solution.py:102
  158.5 0.0 all-reduce.6.cloned.1.call-start
  158.5 0.1 multiply_bitcast_fusion.1
  158.6 0.7 pad_maximum_fusion
  159.4 0.0 all-reduce.6.cloned.1.call-update
  159.4 0.1 broadcast_multiply_fusion
  159.5 39.8 %all-reduce.3 = (f32[8,32]{1,0:T(8,128)S(1)}, f32[8]{0:T(128)S(1)}) all-reduce(f32[8,32]{1,0:T(8,128)S(1)} %broadcast_multiply_fusion, f32[8]{0:T(128)S(1)} %compare_convert_fusion), channel_id=1, replica_groups=mesh['dp'=8,'tm'=4] {'dp','tm'}, use_global_device_ids=true, to_apply=%region_7.8 | all-reduce | flops 264 | bytes 2112 | tf_op jit(solution)/shard_map/psum | solution.py:89
  199.3 0.7 broadcast_divide_fusion
  200.0 0.2 fusion.18
  200.2 1.1 fusion.14
  201.4 91.1 %all-reduce.6.cloned.1.call-done = f32[2,1024,32]{1,2,0:T(8,128)} async-done(((f32[2,1024,32]{1,2,0:T(8,128)}), f32[2,1024,32]{1,2,0:T(8,128)}) %all-reduce.6.cloned.1.call-update) | async-done | bytes 262160 | tf_op jit(solution)/shard_map/psum | solution.py:89
  292.5 1.7 copy.86
  (29 shorter events, 0.1 us)
Async XLA Ops:
  7.2 80.0 %copy-start = (f32[8,32]{1,0:T(8,128)S(1)}, f32[8,32]{1,0:T(8,128)}, u32[]{:S(2)}) copy-start(f32[8,32]{1,0:T(8,128)} %param.12) | copy-start | bytes 3076
  7.2 50.8 %all-gather.3.cloned.1.call-start = ((), (), s32[]{:S(2)}) async-start(), calls=%async_computation.4 | async-start | bytes 7077888 | tf_op jit(solution)/shard_map/all_gather | solution.py:57
  17.5 20.8 %all-to-all-start = ((bf16[4,2,32768]{2,1,0:T(2,128)(2,1)}), bf16[4,2,32768]{2,1,0:T(2,128)(2,1)S(1)}, u32[]{:S(2)}, u32[]{:S(2)}) async-start(bf16[4,2,32768]{2,1,0:T(2,128)(2,1)} %reshape.366), calls=%async_computation | async-start | bytes 1048576 | tf_op jit(solution)/shard_map/all_to_all | solution.py:61
  23.9 63.8 %all-gather.5.cloned.1.call-start = ((), (), s32[]{:S(2)}) async-start(), calls=%async_computation.5 | async-start | bytes 2359296 | tf_op jit(solution)/shard_map/all_gather | solution.py:58
  74.7 1.6 copy-start.8
  75.4 1.0 copy-start.3
  78.0 23.4 %copy-start.1 = (bf16[1,1,256,1024]{3,2,1,0:T(8,128)(2,1)S(1)}, bf16[1,1,256,1024]{3,2,1,0:T(8,128)(2,1)}, u32[]{:S(2)}) copy-start(bf16[1,1,256,1024]{3,2,1,0:T(8,128)(2,1)} %param.7) | copy-start | bytes 1572868
  81.8 19.6 %all-to-all-start.1 = ((bf16[1,4,1,64,1024]{4,3,2,0,1:T(8,128)(2,1)}), bf16[1,4,1,64,1024]{4,3,2,0,1:T(8,128)(2,1)}, u32[]{:S(2)}, u32[]{:S(2)}) async-start(bf16[1,4,1,64,1024]{4,3,2,0,1:T(8,128)(2,1)} %bitcast.153), calls=%async_computation.1 | async-start | bytes 1048576 | tf_op jit(solution)/shard_map/all_to_all | solution.py:65
  86.4 19.0 %copy-start.5 = (f32[2,1024,32]{1,2,0:T(8,128)S(1)}, f32[2,1024,32]{1,2,0:T(8,128)}, u32[]{:S(2)}) copy-start(f32[2,1024,32]{1,2,0:T(8,128)} %param.11) | copy-start | bytes 786436
  101.4 11.7 %copy-start.11 = (bf16[1024,1024]{1,0:T(8,128)(2,1)S(1)}, bf16[1024,1024]{1,0:T(8,128)(2,1)}, u32[]{:S(2)}) copy-start(bf16[1024,1024]{1,0:T(8,128)(2,1)} %all-gather.5.cloned.1.call-done) | copy-start | bytes 6291460
  104.1 5.5 %collective-permute-start = (f32[1,1,1024]{2,1,0:T(1,128)S(1)}, f32[1,1,1024]{2,1,0:T(1,128)S(1)}, u32[]{:S(2)}, u32[]{:S(2)}) collective-permute-start(f32[1,1,1024]{2,1,0:T(1,128)S(1)} %bitcast.156), channel_id=1, source_target_pairs={{1,0},{2,1},{3,2},{5,4},{6,5},{7,6},{9,8},{10,9},{11,10},{13,12},{... | collective-permute-start | bytes 12296 | tf_op jit(solution)/shard_map/ppermute | solution.py:17
  110.0 3.0 collective-permute-start.1
  114.7 15.8 %all-to-all-start.2 = ((bf16[1,1,4,64,1024]{4,3,1,0,2:T(8,128)(2,1)}), bf16[1,1,4,64,1024]{4,3,1,0,2:T(8,128)(2,1)S(1)}, u32[]{:S(2)}, u32[]{:S(2)}) async-start(bf16[1,1,4,64,1024]{4,3,1,0,2:T(8,128)(2,1)} %bitcast.155), calls=%async_computation.2 | async-start | bytes 1048576 | tf_op jit(solution)/shard_map/all_to_all | solution.py:98
  132.2 2.9 copy-start.4
  132.2 2.9 copy-start.9
  132.2 2.9 copy-start.10
  137.9 1.4 copy-start.7
  139.3 1.2 copy-start.6
  154.9 45.1 %copy-start.2 = (bf16[1,1,256,1024]{3,2,1,0:T(8,128)(2,1)S(1)}, bf16[1,1,256,1024]{3,2,1,0:T(8,128)(2,1)}, u32[]{:S(2)}) copy-start(bf16[1,1,256,1024]{3,2,1,0:T(8,128)(2,1)} %param.7) | copy-start | bytes 1572868
  154.9 45.1 %all-to-all-start.3 = ((bf16[1,4,64,1024]{3,2,0,1:T(8,128)(2,1)}), bf16[1,4,64,1024]{3,2,0,1:T(8,128)(2,1)S(1)}, u32[]{:S(2)}, u32[]{:S(2)}) async-start(bf16[1,4,64,1024]{3,2,0,1:T(8,128)(2,1)} %bitcast.41), calls=%async_computation.3 | async-start | bytes 1048576 | tf_op jit(solution)/shard_map/all_to_all | solution.py:102
  158.5 134.0 %all-reduce.6.cloned.1.call-start = ((), (), s32[]{:S(2)}) async-start(), calls=%async_computation.6 | async-start | bytes 524288 | tf_op jit(solution)/shard_map/psum | solution.py:89
Sparse Core Ops, SparseCore 0:
  9.9 48.1 all-gather.2
  59.9 27.7 all-gather.4
  165.4 127.0 all-reduce.5
where the time goes:
time: 301 us
  waiting for transfers between devices  156 us (52%)
  blocking collectives  39.8 us (13%)
  matrix products  32.2 us (11%)
  starting transfers between devices  21.3 us (7%)
  local copies, waits for them, and re-layouts  20.4 us (7%)
  other arithmetic  16.1 us (5%)
  between operations  14.8 us (5%)
    psum x1, waiting for transfers between devices, local(): lax.psum((pair_part, code_part, count_part), ('dp', 'tm'))  91.1 us
    psum x1, blocking collectives, local(): lax.psum((pair_part, code_part, count_part), ('dp', 'tm'))  39.8 us
    all_gather x1, waiting for transfers between devices, local(): lax.all_gather(w_qkv, 'dp', axis=0, tiled=True)  19.1 us
    all_to_all x1, waiting for transfers between devices, local(): lax.all_to_all(normed, 'tm', split_axis=2, concat_axis=1, tiled=True)  13.7 us
    all_to_all x1, waiting for transfers between devices, local(): lax.all_to_all(lifted, 'tm', split_axis=1, concat_axis=2, tiled=True)  13.7 us
    dot_general x2, matrix products, project(): jnp.dot(normed.reshape(-1, shape[-1]), weight, preferred_element_type=jnp...  11.7 us
    all_to_all x1, waiting for transfers between devices, local(): lax.all_to_all(spread, 'tm', split_axis=2, concat_axis=1, tiled=True)  11.2 us
    dot_general x3, matrix products, attend(): jnp.einsum('cphfg,cgphd->cfphd', weights.astype(jnp.float32), values)  7.25 us
  transfers between devices with their start and end apart: 9, of which 8 were waited for; matrix products, arithmetic and copies ran while one was open for 12% of the time, Pallas kernels for 0%

commit v1 on v0

--- a/solution.py
+++ b/solution.py
@@ -9,6 +9,11 @@
 PATCHES = 256
 EPS = 1e-06
 BETA = 0.25
+
+
+def axis_by_axis(x, axis_one, axis_two):
+    half = lax.psum(x, axis_one)
+    return lax.psum(half, axis_two)
 
 
 def passed_along(value, axis, by):
@@ -86,7 +91,7 @@
     )
     code_part = jnp.dot(onehot.T, d_quant, precision=highest)
     count_part = jnp.sum(onehot, axis=0)
-    grad_pair, code_total, count = lax.psum((pair_part, code_part, count_part), ("dp", "tm"))
+    grad_pair, code_total, count = axis_by_axis((pair_part, code_part, count_part), "tm", "dp")
     codebook_step = code_total / count[:, None]
     d_own = jnp.dot(d_action, w_pair[0].T, precision=highest).reshape(pooled.shape)
     d_next = jnp.dot(d_action, w_pair[1].T, precision=highest).reshape(pooled.shape)

time: 301 us -> 264 us (0.88)
  waiting for transfers between devices: 156 us -> 134 us
  blocking collectives: 39.8 us -> 25 us
    psum x1 -> x2, waiting for transfers between devices: 91.1 us -> 68.6 us  [the longest x1 55.3 us: axis_by_axis(): return lax.psum(half, axis_two)]
    psum x1 -> x2, blocking collectives: 39.8 us -> 25 us  [the longest x1 12.7 us: axis_by_axis(): half = lax.psum(x, axis_one)]
  transfers between devices with their start and end apart: 9 -> 10, of which waited for: 8 -> 9; matrix products, arithmetic and copies ran while one was open for 12% -> 14% of each run, Pallas kernels for 0% -> 0%
where the time goes in v1:
time: 264 us; the launch traced here: 263 us
  waiting for transfers between devices  134 us (51%)
  matrix products  32.2 us (12%)
  blocking collectives  25 us (9%)
  starting transfers between devices  21.3 us (8%)
  local copies, waits for them, and re-layouts  20.4 us (8%)
  other arithmetic  16.1 us (6%)
  between operations  14.8 us (6%)
    psum x1, waiting for transfers between devices, axis_by_axis(): return lax.psum(half, axis_two)  55.3 us
    all_gather x1, waiting for transfers between devices, local(): lax.all_gather(w_qkv, 'dp', axis=0, tiled=True)  19.1 us
    all_to_all x1, waiting for transfers between devices, local(): lax.all_to_all(normed, 'tm', split_axis=2, concat_axis=1, tiled=True)  13.7 us
    all_to_all x1, waiting for transfers between devices, local(): lax.all_to_all(lifted, 'tm', split_axis=1, concat_axis=2, tiled=True)  13.7 us
    psum x1, waiting for transfers between devices, axis_by_axis(): half = lax.psum(x, axis_one)  13.3 us
    psum x1, blocking collectives, axis_by_axis(): half = lax.psum(x, axis_one)  12.7 us
    psum x1, blocking collectives, axis_by_axis(): return lax.psum(half, axis_two)  12.3 us
    dot_general x2, matrix products, project(): jnp.dot(normed.reshape(-1, shape[-1]), weight, preferred_element_type=jnp...  11.7 us
  transfers between devices with their start and end apart: 10, of which 9 were waited for; matrix products, arithmetic and copies ran while one was open for 14% of the time, Pallas kernels for 0%

profile of v1, /device:TPU:0, one launch (start us, length us, event | category | flops | bytes accessed | tf_op | source)
XLA Modules:
  0.0 263.4 jit_solution(7530957886521481196)
XLA Ops:
  7.2 0.0 all-gather.3.cloned.1.call-start
  7.2 0.7 all-gather.3.cloned.1.call-update
  7.9 0.7 convert_element_type.110
  8.6 1.2 fusion.15
  9.8 1.2 fusion.17
  11.1 0.8 copy.83
  11.9 0.5 broadcast.182
  12.4 3.9 %reduce.9 = bf16[256,1024]{1,0:T(8,128)(2,1)S(1)} reduce(bf16[256,1,1,1024]{3,2,1,0:T(2,128)(2,1)S(1)} %bitcast.152, bf16[]{:T(256)} %broadcast.182), dimensions={1,2}, to_apply=%bitcast.147.reduce_sub_computation | reduce | bytes 1048578
  16.4 1.2 reshape.366
  17.5 6.3 %all-to-all-start = ((bf16[4,2,32768]{2,1,0:T(2,128)(2,1)}), bf16[4,2,32768]{2,1,0:T(2,128)(2,1)S(1)}, u32[]{:S(2)}, u32[]{:S(2)}) async-start(bf16[4,2,32768]{2,1,0:T(2,128)(2,1)} %reshape.366), calls=%async_computation | async-start | bytes 1048576 | tf_op jit(solution)/shard_map/all_to_all | solution.py:66
  23.9 0.7 all-gather.5.cloned.1.call-update
  24.6 13.7 %all-to-all-done = bf16[4,2,32768]{2,1,0:T(2,128)(2,1)S(1)} async-done(((bf16[4,2,32768]{2,1,0:T(2,128)(2,1)}), bf16[4,2,32768]{2,1,0:T(2,128)(2,1)S(1)}, u32[]{:S(2)}, u32[]{:S(2)}) %all-to-all-start) | async-done | bytes 524320 | tf_op jit(solution)/shard_map/all_to_all | solution.py:66
  38.4 0.5 reshape.367
  38.9 19.1 %all-gather.3.cloned.1.call-done = bf16[1024,3072]{1,0:T(8,128)(2,1)} async-done(((bf16[128,3072]{1,0:T(8,128)(2,1)}), bf16[1024,3072]{1,0:T(8,128)(2,1)}) %all-gather.3.cloned.1.call-update) | async-done | bytes 6291472 | tf_op jit(solution)/shard_map/all_gather | solution.py:62
  58.0 5.8 %convolution_convert_fusion = bf16[256,3072]{1,0:T(8,128)(2,1)} fusion(bf16[1024,3072]{1,0:T(8,128)(2,1)} %all-gather.3.cloned.1.call-done, bf16[1,1,256,1024]{3,1,0,2:T(2,128)(2,1)S(1)} %bitcast.154), kind=kOutput, calls=%fused_computation.1 | convolution fusion | flops 1611399168 | bytes 8388608 | tf_op jit(solution)/shard_map/jvp()/dot_general | solution.py:32
  63.8 3.7 %reshape.339 = bf16[1,4,64,3,16,64]{5,4,3,2,1,0:T(8,128)(2,1)S(1)} reshape(bf16[256,3072]{1,0:T(8,128)(2,1)} %convolution_convert_fusion) | data formatting | bytes 3145728 | tf_op jit(solution)/shard_map/jvp()/reshape;jvp()/reshape | solution.py:39
  67.5 1.9 fusion.43
  69.4 5.3 %fusion.44 = (f32[64,16,4]{2,1,0:T(8,128)S(1)}, f32[64,16,4,4]{2,3,1,0:T(4,128)S(1)}) fusion(pred[4,4]{0,1:T(4,128)(4,1)S(1)} %iota_compare_fusion, bf16[1,4,64,1,16,64]{5,4,3,2,1,0:T(8,128)(2,1)} %get-tuple-element.8, bf16[1,4,64,1,16,64]{5,4,3,2,1,0:T(8,128)(2,1)} %get-tuple-element.9), kind=kOutput, calls=%fused_computation.88 | convolution fusion | flops 2162691 | bytes 1130512 | tf_op jit(solution)/shard_map/jvp()/sub | solution.py:46
  74.8 0.6 divide_convert_fusion
  75.4 1.0 copy-done.3
  76.4 1.6 fusion.5
  78.0 1.2 copy.40
  79.2 2.6 convert_element_type.117
  81.8 4.6 %all-to-all-start.1 = ((bf16[1,4,1,64,1024]{4,3,2,0,1:T(8,128)(2,1)}), bf16[1,4,1,64,1024]{4,3,2,0,1:T(8,128)(2,1)}, u32[]{:S(2)}, u32[]{:S(2)}) async-start(bf16[1,4,1,64,1024]{4,3,2,0,1:T(8,128)(2,1)} %bitcast.153), calls=%async_computation.1 | async-start | bytes 1048576 | tf_op jit(solution)/shard_map/all_to_all | solution.py:70
  87.1 0.1 convolution_bitcast_fusion.3
  87.2 0.5 all-gather.5.cloned.1.call-done
  87.7 13.7 %all-to-all-done.1 = bf16[1,4,1,64,1024]{4,3,2,0,1:T(8,128)(2,1)} async-done(((bf16[1,4,1,64,1024]{4,3,2,0,1:T(8,128)(2,1)}), bf16[1,4,1,64,1024]{4,3,2,0,1:T(8,128)(2,1)}, u32[]{:S(2)}, u32[]{:S(2)}) %all-to-all-start.1) | async-done | bytes 524320 | tf_op jit(solution)/shard_map/all_to_all | solution.py:70
  101.4 2.6 fusion.9
  104.1 1.3 collective-permute-start
  105.4 0.2 convolution_bitcast_fusion.5
  105.6 4.0 %collective-permute-done = f32[1,1,1024]{2,1,0:T(1,128)S(1)} collective-permute-done((f32[1,1,1024]{2,1,0:T(1,128)S(1)}, f32[1,1,1024]{2,1,0:T(1,128)S(1)}, u32[]{:S(2)}, u32[]{:S(2)}) %collective-permute-start) | collective-permute-done | bytes 4128 | tf_op jit(solution)/shard_map/ppermute | solution.py:22
  109.6 0.2 broadcast_multiply_fusion.2
  109.8 0.2 convolution_bitcast_fusion.1
  110.0 1.7 collective-permute-start.1
  111.6 1.3 collective-permute-done.1
  113.0 0.2 fusion.10
  113.1 1.6 convolution_convert_fusion.7
  114.7 3.7 %all-to-all-start.2 = ((bf16[1,1,4,64,1024]{4,3,1,0,2:T(8,128)(2,1)}), bf16[1,1,4,64,1024]{4,3,1,0,2:T(8,128)(2,1)S(1)}, u32[]{:S(2)}, u32[]{:S(2)}) async-start(bf16[1,1,4,64,1024]{4,3,1,0,2:T(8,128)(2,1)} %bitcast.155), calls=%async_computation.2 | async-start | bytes 1048576 | tf_op jit(solution)/shard_map/all_to_all | solution.py:103
  118.4 0.9 multiply_divide_fusion
  119.3 11.2 %all-to-all-done.2 = bf16[1,1,4,64,1024]{4,3,1,0,2:T(8,128)(2,1)S(1)} async-done(((bf16[1,1,4,64,1024]{4,3,1,0,2:T(8,128)(2,1)}), bf16[1,1,4,64,1024]{4,3,1,0,2:T(8,128)(2,1)S(1)}, u32[]{:S(2)}, u32[]{:S(2)}) %all-to-all-start.2) | async-done | bytes 524320 | tf_op jit(solution)/shard_map/all_to_all | solution.py:103
  130.5 1.7 reshape.349
  132.2 2.9 %fusion.6 = bf16[1,4,64,1,16,64]{5,1,4,2,3,0:T(4,128)(2,1)S(1)} fusion(bf16[64,16,4,4]{2,3,1,0:T(4,128)(2,1)} %copy-done.3, bf16[1,4,64,16,64]{4,3,2,1,0:T(8,128)(2,1)} %reshape.349), kind=kOutput, calls=%fused_computation.26 | convolution fusion | flops 2359296 | bytes 1081344 | tf_op jit(solution)/shard_map/transpose(jvp(cphfg,cgphd->cfphd))/dot_general | solution.py:47
  135.1 2.7 %fusion.4 = (f32[64,16,4]{2,1,0:T(8,128)S(1)}, bf16[64,16,4,4]{2,3,1,0:T(4,128)(2,1)S(1)}) fusion(f32[64,16,4,4]{2,3,1,0:T(4,128)S(1)} %get-tuple-element.15, f32[64,16,4]{2,1,0:T(8,128)S(1)} %copy-done.10, bf16[1,4,64,1,16,64]{5,4,3,2,1,0:T(8,128)(2,1)S(1)} %copy-done.9, bf16[1,4,64,16,64]{4,3,2,1,0:T(8,128)(2,1)S(1)} %copy-done.4), kind=kOutput, calls=%fused_computation.8 | convolution fusion | flops 2174976 | bytes 1179648 | tf_op jit(solution)/shard_map/transpose(jvp(cphfg,cgphd->cfphd))/dot_general | solution.py:47
  137.9 1.4 select_multiply_fusion
  139.3 1.2 fusion.7
  140.5 1.6 fusion.8
  142.2 3.1 %pad_add_fusion = bf16[1,4,64,3,16,64]{5,1,4,2,3,0:T(4,128)(2,1)S(1)} fusion(bf16[1,4,64,1,16,64]{5,1,4,2,3,0:T(4,128)(2,1)S(1)} %fusion.8, bf16[1,4,64,1,16,64]{5,1,4,2,3,0:T(4,128)(2,1)S(1)} %fusion.7, bf16[1,4,64,1,16,64]{5,1,4,2,3,0:T(4,128)(2,1)S(1)} %fusion.6), kind=kLoop, calls=%fused_computation.2 | loop fusion | flops 1572864 | bytes 3145728 | tf_op jit(solution)/shard_map/transpose(jvp())/add_any | solution.py:40
  145.3 0.4 copy.45
  145.7 3.2 %reshape.351 = bf16[256,3072]{1,0:T(8,128)(2,1)} reshape(bf16[1,4,64,3,16,64]{5,4,3,2,1,0:T(8,128)(2,1)S(1)} %copy.45) | data formatting | bytes 3145728 | tf_op jit(solution)/shard_map/transpose(jvp())/reshape;transpose(jvp())/reshape | solution.py:33
  149.0 5.9 %convolution_convert_fusion.6 = bf16[256,1024]{1,0:T(8,128)(2,1)} fusion(bf16[256,3072]{1,0:T(8,128)(2,1)} %reshape.351, bf16[1024,3072]{1,0:T(8,128)(2,1)} %all-gather.3.cloned.1.call-done), kind=kOutput, calls=%fused_computation.29 | convolution fusion | flops 1610874880 | bytes 8388608 | tf_op jit(solution)/shard_map/transpose(jvp())/dot_general | solution.py:32
  154.8 3.6 %all-to-all-start.3 = ((bf16[1,4,64,1024]{3,2,0,1:T(8,128)(2,1)}), bf16[1,4,64,1024]{3,2,0,1:T(8,128)(2,1)S(1)}, u32[]{:S(2)}, u32[]{:S(2)}) async-start(bf16[1,4,64,1024]{3,2,0,1:T(8,128)(2,1)} %bitcast.41), calls=%async_computation.3 | async-start | bytes 1048576 | tf_op jit(solution)/shard_map/all_to_all | solution.py:107
  158.5 0.0 all-reduce.8.cloned.1.call-start
  158.5 0.1 multiply_bitcast_fusion.1
  158.6 0.7 pad_maximum_fusion
  159.3 0.0 all-reduce.10.cloned.1.call-start
  159.4 0.1 broadcast_multiply_fusion
  159.5 12.7 %all-reduce.4 = (f32[8,32]{1,0:T(8,128)S(1)}, f32[8]{0:T(128)S(1)}) all-reduce(f32[8,32]{1,0:T(8,128)S(1)} %broadcast_multiply_fusion, f32[8]{0:T(128)S(1)} %compare_convert_fusion), channel_id=1, replica_groups=mesh['dp'=8,'tm'=4] {'tm'}, use_global_device_ids=true, to_apply=%region_8.9 | all-reduce | flops 264 | bytes 2112 | tf_op jit(solution)/shard_map/psum | solution.py:15
  172.2 12.3 %all-reduce.3 = (f32[8,32]{1,0:T(8,128)S(1)}, f32[8]{0:T(128)S(1)}) all-reduce(f32[8,32]{1,0:T(8,128)S(1)} %get-tuple-element.5, f32[8]{0:T(128)S(1)} %get-tuple-element.6), channel_id=1, replica_groups=mesh['dp'=8,'tm'=4] {'dp'}, use_global_device_ids=true, to_apply=%region_9.10 | all-reduce | flops 264 | bytes 2112 | tf_op jit(solution)/shard_map/psum | solution.py:16
  184.5 0.7 broadcast_divide_fusion
  185.2 13.3 %all-reduce.8.cloned.1.call-done = f32[2,1024,32]{1,2,0:T(8,128)} async-done(((f32[2,1024,32]{1,2,0:T(8,128)}), f32[2,1024,32]{1,2,0:T(8,128)}) %all-reduce.8.cloned.1.call-update) | async-done | bytes 262160 | tf_op jit(solution)/shard_map/psum | solution.py:15
  198.6 0.3 fusion.18
  198.8 1.1 fusion.14
  200.0 55.3 %all-reduce.10.cloned.1.call-done = f32[2,1024,32]{1,2,0:T(8,128)} async-done(((f32[2,1024,32]{1,2,0:T(8,128)}), f32[2,1024,32]{1,2,0:T(8,128)}) %all-reduce.10.cloned.1.call-update) | async-done | bytes 262160 | tf_op jit(solution)/shard_map/psum | solution.py:16
  255.2 1.7 copy.87
  (33 shorter events, 0.2 us)
Async XLA Ops:
  7.2 79.9 %copy-start = (f32[8,32]{1,0:T(8,128)S(1)}, f32[8,32]{1,0:T(8,128)}, u32[]{:S(2)}) copy-start(f32[8,32]{1,0:T(8,128)} %param.12) | copy-start | bytes 3076
  7.2 50.8 %all-gather.3.cloned.1.call-start = ((), (), s32[]{:S(2)}) async-start(), calls=%async_computation.4 | async-start | bytes 7077888 | tf_op jit(solution)/shard_map/all_gather | solution.py:62
  17.5 20.8 %all-to-all-start = ((bf16[4,2,32768]{2,1,0:T(2,128)(2,1)}), bf16[4,2,32768]{2,1,0:T(2,128)(2,1)S(1)}, u32[]{:S(2)}, u32[]{:S(2)}) async-start(bf16[4,2,32768]{2,1,0:T(2,128)(2,1)} %reshape.366), calls=%async_computation | async-start | bytes 1048576 | tf_op jit(solution)/shard_map/all_to_all | solution.py:66
  23.9 63.8 %all-gather.5.cloned.1.call-start = ((), (), s32[]{:S(2)}) async-start(), calls=%async_computation.5 | async-start | bytes 2359296 | tf_op jit(solution)/shard_map/all_gather | solution.py:63
  74.8 1.6 copy-start.8
  75.4 1.0 copy-start.3
  78.0 23.4 %copy-start.1 = (bf16[1,1,256,1024]{3,2,1,0:T(8,128)(2,1)S(1)}, bf16[1,1,256,1024]{3,2,1,0:T(8,128)(2,1)}, u32[]{:S(2)}) copy-start(bf16[1,1,256,1024]{3,2,1,0:T(8,128)(2,1)} %param.7) | copy-start | bytes 1572868
  81.8 19.6 %all-to-all-start.1 = ((bf16[1,4,1,64,1024]{4,3,2,0,1:T(8,128)(2,1)}), bf16[1,4,1,64,1024]{4,3,2,0,1:T(8,128)(2,1)}, u32[]{:S(2)}, u32[]{:S(2)}) async-start(bf16[1,4,1,64,1024]{4,3,2,0,1:T(8,128)(2,1)} %bitcast.153), calls=%async_computation.1 | async-start | bytes 1048576 | tf_op jit(solution)/shard_map/all_to_all | solution.py:70
  86.4 19.0 %copy-start.5 = (f32[2,1024,32]{1,2,0:T(8,128)S(1)}, f32[2,1024,32]{1,2,0:T(8,128)}, u32[]{:S(2)}) copy-start(f32[2,1024,32]{1,2,0:T(8,128)} %param.11) | copy-start | bytes 786436
  101.4 11.7 %copy-start.11 = (bf16[1024,1024]{1,0:T(8,128)(2,1)S(1)}, bf16[1024,1024]{1,0:T(8,128)(2,1)}, u32[]{:S(2)}) copy-start(bf16[1024,1024]{1,0:T(8,128)(2,1)} %all-gather.5.cloned.1.call-done) | copy-start | bytes 6291460
  104.1 5.5 %collective-permute-start = (f32[1,1,1024]{2,1,0:T(1,128)S(1)}, f32[1,1,1024]{2,1,0:T(1,128)S(1)}, u32[]{:S(2)}, u32[]{:S(2)}) collective-permute-start(f32[1,1,1024]{2,1,0:T(1,128)S(1)} %bitcast.156), channel_id=1, source_target_pairs={{1,0},{2,1},{3,2},{5,4},{6,5},{7,6},{9,8},{10,9},{11,10},{13,12},{... | collective-permute-start | bytes 12296 | tf_op jit(solution)/shard_map/ppermute | solution.py:22
  110.0 3.0 %collective-permute-start.1 = (f32[1,1,1024]{2,1,0:T(1,128)S(1)}, f32[1,1,1024]{2,1,0:T(1,128)S(1)}, u32[]{:S(2)}, u32[]{:S(2)}) collective-permute-start(f32[1,1,1024]{2,1,0:T(1,128)S(1)} %convolution_bitcast_fusion.1), channel_id=1, source_target_pairs={{0,1},{1,2},{2,3},{4,5},{5,6},{6,7},{8,9},{9,10},{10,11},{12,13},{... | collective-permute-start | bytes 12296 | tf_op jit(solution)/shard_map/ppermute | solution.py:22
  114.7 15.8 %all-to-all-start.2 = ((bf16[1,1,4,64,1024]{4,3,1,0,2:T(8,128)(2,1)}), bf16[1,1,4,64,1024]{4,3,1,0,2:T(8,128)(2,1)S(1)}, u32[]{:S(2)}, u32[]{:S(2)}) async-start(bf16[1,1,4,64,1024]{4,3,1,0,2:T(8,128)(2,1)} %bitcast.155), calls=%async_computation.2 | async-start | bytes 1048576 | tf_op jit(solution)/shard_map/all_to_all | solution.py:103
  132.1 2.9 %copy-start.4 = (bf16[1,4,64,16,64]{4,3,2,1,0:T(8,128)(2,1)S(1)}, bf16[1,4,64,16,64]{4,3,2,1,0:T(8,128)(2,1)}, u32[]{:S(2)}) copy-start(bf16[1,4,64,16,64]{4,3,2,1,0:T(8,128)(2,1)} %reshape.349) | copy-start | bytes 1572868
  132.1 2.9 %copy-start.9 = (bf16[1,4,64,1,16,64]{5,4,3,2,1,0:T(8,128)(2,1)S(1)}, bf16[1,4,64,1,16,64]{5,4,3,2,1,0:T(8,128)(2,1)}, u32[]{:S(2)}) copy-start(bf16[1,4,64,1,16,64]{5,4,3,2,1,0:T(8,128)(2,1)} %get-tuple-element.7) | copy-start | bytes 1572868
  132.2 3.0 %copy-start.10 = (f32[64,16,4]{2,1,0:T(8,128)S(1)}, f32[64,16,4]{2,1,0:T(8,128)}, u32[]{:S(2)}) copy-start(f32[64,16,4]{2,1,0:T(8,128)} %multiply_divide_fusion) | copy-start | bytes 49156
  137.9 1.4 copy-start.7
  139.3 1.2 copy-start.6
  154.8 43.7 %copy-start.2 = (bf16[1,1,256,1024]{3,2,1,0:T(8,128)(2,1)S(1)}, bf16[1,1,256,1024]{3,2,1,0:T(8,128)(2,1)}, u32[]{:S(2)}) copy-start(bf16[1,1,256,1024]{3,2,1,0:T(8,128)(2,1)} %param.7) | copy-start | bytes 1572868
  154.8 43.7 %all-to-all-start.3 = ((bf16[1,4,64,1024]{3,2,0,1:T(8,128)(2,1)}), bf16[1,4,64,1024]{3,2,0,1:T(8,128)(2,1)S(1)}, u32[]{:S(2)}, u32[]{:S(2)}) async-start(bf16[1,4,64,1024]{3,2,0,1:T(8,128)(2,1)} %bitcast.41), calls=%async_computation.3 | async-start | bytes 1048576 | tf_op jit(solution)/shard_map/all_to_all | solution.py:107
  158.5 40.1 %all-reduce.8.cloned.1.call-start = ((), (), s32[]{:S(2)}) async-start(), calls=%async_computation.6 | async-start | bytes 524288 | tf_op jit(solution)/shard_map/psum | solution.py:15
  159.3 95.9 %all-reduce.10.cloned.1.call-start = ((), (), s32[]{:S(2)}) async-start(), calls=%async_computation.7 | async-start | bytes 524288 | tf_op jit(solution)/shard_map/psum | solution.py:16
Sparse Core Ops, SparseCore 0:
  9.9 48.1 all-gather.2
  59.9 27.7 all-gather.4
  162.2 36.3 all-reduce.7
  201.4 53.7 all-reduce.9
